TPU v7x, 32 devices: a whole 2x2x4 slice. The times are simulated.
32 devices in a mesh: gx: 4 (over y, x), gy: 4 (over z), gz: 2 (over core).
Axes of the slice: x: 2, y: 2, z: 4, core: 2. Of those that a mesh axis runs over, the one named last changes fastest.
Arguments:
- displacement: float32 [4, 4, 9216], P('gx', 'gy', 'gz'), may hold values from -0.1 to 0.1
- species: int32 [4, 4, 3072], P('gx', 'gy', 'gz'), may hold values from 0 to 1
- centres: int32 [4, 4, 32], P('gx', 'gy', 'gz'), may hold values from 0 to 1535, as said below
- neighbours: int32 [4, 4, 1024], P('gx', 'gy', 'gz'), may hold values from 0 to 5183, as said below
- neighbour_count: int32 [4, 4, 32], P('gx', 'gy', 'gz'), may hold values from 1 to 32, as said below
- live_centres: int32 [4, 4, 2], P('gx', 'gy', 'gz'), may hold values from 8 to 16, as said below
- w_two: float32 [12, 64], replicated, may hold values from -1.75 to 1.75
- w_lat: float32 [64, 64], replicated, may hold values from -0.75 to 0.75
- w_env: float32 [64, 64], replicated, may hold values from -0.75 to 0.75
- w_out: float32 [256, 64], replicated, may hold values from -0.375 to 0.375
- readout: float32 [64], replicated, may hold values from -0.75 to 0.75
Outputs:
- centre_energy: float32 [4, 4, 32], P('gx', 'gy', 'gz')
- forces: float32 [4, 4, 9216], P('gx', 'gy', 'gz')
Inputs may be any that keep to these rules, and one draw needn't show every extreme that they name: `centres`: local atom index of an owned atom; entries may repeat. `neighbours`: extended index of an atom whose cell lies within two cells of the centre's cell in each dimension, with squared cell distance at most 4; never the centre itself. `neighbour_count`: in every domain some centre has all 32 slots live. `live_centres`: some domain has all 16 centres live; the live centres are the first ones.
All inputs are finite; a program needn't handle non-finite values.
Results may differ from a plain program's by a relative error of at most 0.0003.
Values sent between devices are 32-bit elements; how exact they have to be, the bound alone decides.
A program may use at most 64 MiB of HBM per device.

v0:
```python
import math

import jax
import jax.numpy as jnp
import numpy as np
from jax import lax
from jax.sharding import PartitionSpec as P

CELLS = 8
NBASIS = 8
SPECIES = 2


cutoff = 6.0
cell_side = 3.1
env_scale = 0.2
block_limit = 64
site_rows = np.array([[0.25, 0.25, 0.25], [0.75, 0.75, 0.25], [0.25, 0.75, 0.75]], np.float32)


def shifted(shard, axis, by):
    length = lax.axis_size(axis)
    return lax.ppermute(shard, axis, [(i, (i + by) % length) for i in range(length)])


def with_halo(shard, sides, width):
    for axis, dim in sides:
        size, length = (lax.axis_size(axis), shard.shape[dim])
        up = [(i, (i + 1) % size) for i in range(size)]
        down = [(j, i) for i, j in up]
        last = lax.slice_in_dim(shard, length - width, length, axis=dim)
        first = lax.slice_in_dim(shard, 0, width, axis=dim)
        before = lax.ppermute(last, axis, up)
        after = lax.ppermute(first, axis, down)
        shard = jnp.concatenate([before, shard, after], axis=dim)
    return shard


def mixing(weight, data):
    return jnp.dot(
        weight.T, data, precision=lax.Precision.HIGHEST, preferred_element_type=jnp.float32
    )


def harmonics(unit):
    ux, uy, uz = (unit[0], unit[1], unit[2])
    root3 = math.sqrt(3.0)
    root5 = math.sqrt(5.0)
    root15 = math.sqrt(15.0)
    return jnp.stack(
        [
            jnp.ones_like(ux),
            root3 * ux,
            root3 * uy,
            root3 * uz,
            root15 * ux * uy,
            root15 * uy * uz,
            0.5 * root5 * (3.0 * uz * uz - 1.0),
            root15 * ux * uz,
            0.5 * root15 * (ux * ux - uy * uy),
        ],
        0,
    )


def block_energy(rvec, kind_first, kind_second, live, w_two, w_lat, w_env, w_out, readout, slots):
    dist = jnp.sqrt(jnp.sum(rvec * rvec, axis=0))
    unit = rvec / dist
    ratio = dist / cutoff
    envelope = jnp.where(
        ratio < 1.0, 1.0 - 28.0 * ratio**6 + 48.0 * ratio**7 - 21.0 * ratio**8, 0.0
    )
    orders = jnp.arange(1, NBASIS + 1, dtype=jnp.float32)[:, None]
    basis = (
        math.sqrt(2.0 / cutoff)
        * jnp.sin(orders * math.pi * dist[None, :] / cutoff)
        / dist[None, :]
        * envelope[None, :]
    )
    kinds = jnp.arange(SPECIES, dtype=jnp.float32)[:, None]
    first_hot = (kind_first[None, :] == kinds).astype(jnp.float32)
    second_hot = (kind_second[None, :] == kinds).astype(jnp.float32)
    inputs = jnp.concatenate([first_hot, second_hot, basis], 0)
    hidden = jax.nn.silu(mixing(w_two, inputs))
    latent = jax.nn.silu(mixing(w_lat, hidden))
    weights = mixing(w_env, latent) * (envelope * live)[None, :]
    harm = harmonics(unit)
    width = latent.shape[0]
    centre_total = rvec.shape[1] // slots
    edge = (harm[:, None, :] * weights[None, :, :]).reshape(9, width, centre_total, slots)
    environ = env_scale * jnp.sum(edge, axis=3)
    product = edge * environ[:, :, :, None]
    scalars = jnp.stack(
        [product[0], jnp.sum(product[1:4], axis=0), jnp.sum(product[4:9], axis=0)], 0
    )
    joined = jnp.concatenate([latent, scalars.reshape(3 * width, centre_total * slots)], 0)
    updated = jax.nn.silu(mixing(w_out, joined))
    pair_energy = jnp.dot(readout, updated, precision=lax.Precision.HIGHEST) * envelope * live
    return jnp.sum(pair_energy.reshape(centre_total, slots), axis=1)


def along_gx(values, by):
    return shifted(values, "gx", by)


def along_gy(values, by):
    return shifted(values, "gy", by)


def along_gz(values, by):
    return shifted(values, "gz", by)


def fold_layers(values, axis_dim, mover):
    length = values.shape[axis_dim]
    inner_len = length - 4
    from_above = mover(lax.slice_in_dim(values, 0, 2, axis=axis_dim), -1)
    from_below = mover(lax.slice_in_dim(values, length - 2, length, axis=axis_dim), 1)
    inner = lax.slice_in_dim(values, 2, length - 2, axis=axis_dim)
    widths_low = [(0, 0)] * values.ndim
    widths_high = [(0, 0)] * values.ndim
    widths_low[axis_dim] = (0, inner_len - 2)
    widths_high[axis_dim] = (inner_len - 2, 0)
    return inner + jnp.pad(from_below, widths_low) + jnp.pad(from_above, widths_high)


def local(
    displacement,
    species,
    centres,
    neighbours,
    neighbour_count,
    live_centres,
    w_two,
    w_lat,
    w_env,
    w_out,
    readout,
):
    side_x = CELLS
    side_y = CELLS
    side_z = CELLS
    cells = jnp.concatenate(
        [
            displacement.reshape(side_x, side_y, side_z, 9),
            species.reshape(side_x, side_y, side_z, 3).astype(jnp.float32),
        ],
        axis=3,
    )
    padded = with_halo(cells, (("gx", 0), ("gy", 1), ("gz", 2)), 2)
    ext_x, ext_y, ext_z = (side_x + 4, side_y + 4, side_z + 4)
    total_ext = ext_x * ext_y * ext_z * 3
    shifts = padded[..., :9].reshape(ext_x, ext_y, ext_z, 3, 3)
    kinds = padded[..., 9:].reshape(1, total_ext)
    grid_x = jnp.arange(ext_x, dtype=jnp.float32)[:, None, None] - 2.0
    grid_y = jnp.arange(ext_y, dtype=jnp.float32)[None, :, None] - 2.0
    grid_z = jnp.arange(ext_z, dtype=jnp.float32)[None, None, :] - 2.0
    corner = jnp.stack(jnp.broadcast_arrays(grid_x, grid_y, grid_z), -1)
    sites = jnp.array(site_rows, dtype=jnp.float32)
    places = (corner[:, :, :, None, :] + sites[None, None, None, :, :] + shifts) * cell_side
    table = jnp.concatenate([places.reshape(total_ext, 3).T, kinds], 0)
    centre_list = centres.reshape(-1)
    centre_total = centre_list.shape[0]
    neighbour_list = neighbours.reshape(-1)
    slots = neighbour_list.shape[0] // centre_total
    count_list = neighbour_count.reshape(-1)
    alive = live_centres.reshape(())
    atom_first = centre_list % 3
    cell_first = centre_list // 3
    loc_z = cell_first % side_z
    loc_y = cell_first // side_z % side_y
    loc_x = cell_first // (side_z * side_y)
    first_ext = (((loc_x + 2) * ext_y + loc_y + 2) * ext_z + loc_z + 2) * 3 + atom_first
    slot_ids = jnp.arange(slots, dtype=jnp.int32)
    block_centres = min(block_limit, centre_total)

    def one_block(block, carry):
        forces, energies = carry
        start = block * block_centres
        first = jnp.repeat(first_ext, slots)
        rows_first = jnp.take(table, first, axis=1)
        rows_second = jnp.take(table, neighbour_list, axis=1)
        rvec = rows_second[:3] - rows_first[:3]
        centre_ids = start + jnp.arange(block_centres, dtype=jnp.int32)
        live = (
            ((slot_ids[None, :] < count_list[:, None]) & (centre_ids[:, None] < alive))
            .reshape(-1)
            .astype(jnp.float32)
        )

        def energy_of(vectors):
            return block_energy(
                vectors,
                rows_first[3],
                rows_second[3],
                live,
                w_two,
                w_lat,
                w_env,
                w_out,
                readout,
                slots,
            )

        energy, pullback = jax.vjp(energy_of, rvec)
        grad = pullback(jnp.ones_like(energy))[0]
        forces = forces.at[:, neighbour_list].add(-grad)
        forces = forces.at[:, first].add(grad)
        energies = lax.dynamic_update_slice_in_dim(energies, energy, start, 0)
        return (forces, energies)

    initial = (jnp.zeros((3, total_ext), jnp.float32), jnp.zeros((centre_total,), jnp.float32))
    block_total = centre_total // block_centres
    forces, energies = lax.fori_loop(0, block_total, one_block, initial)
    grid_forces = jnp.transpose(forces.reshape(3, ext_x, ext_y, ext_z, 3), (1, 2, 3, 4, 0)).reshape(
        ext_x, ext_y, ext_z, 9
    )
    owned = fold_layers(
        fold_layers(fold_layers(grid_forces, 0, along_gx), 1, along_gy), 2, along_gz
    )
    return (energies.reshape(1, 1, centre_total), owned.reshape(1, 1, side_x * side_y * side_z * 9))


def solution(mesh):
    in_specs = (
        P("gx", "gy", "gz"),
        P("gx", "gy", "gz"),
        P("gx", "gy", "gz"),
        P("gx", "gy", "gz"),
        P("gx", "gy", "gz"),
        P("gx", "gy", "gz"),
        P(),
        P(),
        P(),
        P(),
        P(),
    )
    out_specs = (P("gx", "gy", "gz"), P("gx", "gy", "gz"))
    return jax.shard_map(local, mesh=mesh, in_specs=in_specs, out_specs=out_specs, check_vma=False)
```

profile of v0, /device:TPU:0, one launch (start us, length us, event | category | flops | bytes accessed | tf_op | source)
XLA Modules:
  0.0 80.1 jit_solution(15932010964033137161)
XLA Ops:
  0.6 0.8 %reduce.2 = f32[4608]{0:T(1024)S(1)} reduce(f32[1,1,4608]{2,1,0:T(1,128)} %param.14, f32[]{:T(128)} %constant.201), dimensions={0,1}, to_apply=%param.14.reduce_sub_computation | reduce | bytes 36868 | tf_op args[0]
  1.7 0.7 convert_reduce_fusion
  2.7 3.0 %collective-permute-start = (f32[2,8,8,12]{3,2,1,0:T(8,128)S(1)}, f32[2,8,8,12]{3,2,1,0:T(8,128)S(1)}, u32[]{:S(2)}, u32[]{:S(2)}) collective-permute-start(f32[2,8,8,12]{3,2,1,0:T(8,128)S(1)} %get-tuple-element.68), channel_id=1, source_target_pairs={{0,8},{8,16},{16,24},{24,0},{1,9},{9,17},{17,25},{25,1},{2,10},{10... | collective-permute-start | bytes 18440 | tf_op jit(solution)/shard_map/ppermute | solution.py:33
  5.7 1.0 %collective-permute-start.1 = (f32[2,8,8,12]{3,2,1,0:T(8,128)S(1)}, f32[2,8,8,12]{3,2,1,0:T(8,128)S(1)}, u32[]{:S(2)}, u32[]{:S(2)}) collective-permute-start(f32[2,8,8,12]{3,2,1,0:T(8,128)S(1)} %get-tuple-element.69), channel_id=1, source_target_pairs={{8,0},{16,8},{24,16},{0,24},{9,1},{17,9},{25,17},{1,25},{10,2},{18... | collective-permute-start | bytes 18440 | tf_op jit(solution)/shard_map/ppermute | solution.py:34
  6.8 0.7 fusion.67
  7.6 0.7 compare_select_fusion.2
  8.3 0.7 compare_and_fusion
  9.0 0.7 compare_select_fusion.1
  10.6 3.0 %broadcast_add_fusion = f32[12,12,12,3,3]{3,2,1,0,4:T(8,128)} fusion(f32[3,3]{0,1:T(4,128)} %constant.170.clone, f32[12,12,12,3]{2,1,0,3:T(8,128)S(1)} %pad_maximum_fusion.2), kind=kLoop, calls=%fused_computation.12 | loop fusion | flops 15552 | bytes 82980 | tf_op jit(solution)/shard_map/add | solution.py:160
  13.8 2.0 %collective-permute-start.2 = (f32[12,2,8,12]{3,2,1,0:T(8,128)S(1)}, f32[12,2,8,12]{3,2,1,0:T(8,128)S(1)}, u32[]{:S(2)}, u32[]{:S(2)}) collective-permute-start(f32[12,2,8,12]{3,2,1,0:T(8,128)S(1)} %get-tuple-element.63), channel_id=1, source_target_pairs={{0,2},{2,4},{4,6},{6,0},{1,3},{3,5},{5,7},{7,1},{8,10},{10,12},{12... | collective-permute-start | bytes 27656 | tf_op jit(solution)/shard_map/ppermute | solution.py:33
  15.9 2.1 %collective-permute-start.3 = (f32[12,2,8,12]{3,2,1,0:T(8,128)S(1)}, f32[12,2,8,12]{3,2,1,0:T(8,128)S(1)}, u32[]{:S(2)}, u32[]{:S(2)}) collective-permute-start(f32[12,2,8,12]{3,2,1,0:T(8,128)S(1)} %get-tuple-element.64), channel_id=1, source_target_pairs={{2,0},{4,2},{6,4},{0,6},{3,1},{5,3},{7,5},{1,7},{10,8},{12,10},{14... | collective-permute-start | bytes 27656 | tf_op jit(solution)/shard_map/ppermute | solution.py:34
  18.0 3.5 %collective-permute-done.2 = f32[12,2,8,12]{3,2,1,0:T(8,128)S(1)} collective-permute-done((f32[12,2,8,12]{3,2,1,0:T(8,128)S(1)}, f32[12,2,8,12]{3,2,1,0:T(8,128)S(1)}, u32[]{:S(2)}, u32[]{:S(2)}) %collective-permute-start.2) | collective-permute-done | bytes 9248 | tf_op jit(solution)/shard_map/ppermute | solution.py:33
  22.0 0.5 collective-permute-start.5
  22.5 3.3 %add.194 = f32[5184,3]{0,1:T(4,128)S(1)} reshape(f32[12,12,12,3,3]{3,2,1,0,4:T(8,128)} %broadcast_add_fusion) | data formatting | bytes 124416 | tf_op jit(solution)/shard_map/add | solution.py:160
  26.3 1.4 %slice.152 = f32[12,12,12,3]{3,2,1,0:T(8,128)} slice(f32[12,12,12,12]{3,2,1,0:T(8,128)S(1)} %pad_maximum_fusion), slice={[0:12], [0:12], [0:12], [9:12]} | slice | bytes 41472 | tf_op jit(solution)/shard_map/slice | solution.py:154
  27.7 2.0 %reshape.344 = f32[5184,3]{1,0:T(8,128)S(1)} reshape(f32[12,12,12,9]{3,2,1,0:T(8,128)} %bitcast.94) | data formatting | bytes 124416 | tf_op jit(solution)/shard_map/reshape | solution.py:153
  29.7 0.8 copy.166
  30.5 1.8 %reshape.345 = f32[1,5184]{1,0:T(1,128)S(1)} reshape(f32[12,12,12,3]{3,2,1,0:T(8,128)} %slice.152) | data formatting | bytes 41472 | tf_op jit(solution)/shard_map/reshape | solution.py:154
  32.5 0.8 copy.167
  33.2 1.0 %gather_fusion = f32[512,4]{1,0:T(8,128)S(1)} fusion(f32[4,5184]{0,1:T(8,128)S(1)} %copy.167, s32[1024]{0:T(1024)S(1)} %pad_clamp_fusion.1), kind=kCustom, calls=%fused_computation.clone | custom fusion | bytes 18432 | tf_op jit(solution)/shard_map/while/body/eval_jaxpr/jit(_take)/gather | solution.py:181
  34.4 1.0 %gather_fusion.1 = f32[512,4]{1,0:T(8,128)S(1)} fusion(f32[4,5184]{0,1:T(8,128)S(1)} %copy.167, s32[1024]{0:T(1024)S(1)} %pad_clamp_fusion), kind=kCustom, calls=%fused_computation.1.clone | custom fusion | bytes 18432 | tf_op jit(solution)/shard_map/while/body/eval_jaxpr/jit(_take)/gather | solution.py:182
  37.2 0.9 %multiply_reduce_fusion = f32[9,64,16]{1,2,0:T(8,128)S(1)} fusion(f32[64,16,32]{0,2,1:T(8,128)S(1)} %bitcast.95, f32[9,16,32]{2,1,0:T(8,128)S(1)} %mul.743), kind=kLoop, calls=%fused_computation.6 | loop fusion | flops 580608 | bytes 186368 | tf_op jit(solution)/shard_map/while/body/eval_jaxpr/jvp()/reduce_sum | solution.py:91
  38.1 0.7 multiply_multiply_fusion.1
  39.1 0.5 copy.172
  39.7 0.6 reshape.348
  40.4 0.7 convolution_bitcast_fusion.1
  41.1 0.7 convolution_bitcast_fusion
  42.7 0.9 %fusion = f32[9,64,16]{1,2,0:T(8,128)S(1)} fusion(f32[1,64,16,32]{1,3,2,0:T(8,128)S(1)} %bitcast.99, f32[3,64,16,32]{1,3,2,0:T(8,128)S(1)} %broadcast_in_dim.80, f32[5,64,16,32]{1,3,2,0:T(8,128)S(1)} %broadcast_in_dim.79, f32[64,16,32]{0,2,1:T(8,128)S(1)} %bitcast.97, f32[9,16,32]{2,1,0:T(8,128)S(1)} %mul.743), kind=kLoop, calls=%fused_computation.7 | loop fusion | flops 1465344 | bytes 1366016 | tf_op jit(solution)/shard_map/while/body/eval_jaxpr/transpose(jvp())/reduce_sum | solution.py:92
  43.6 1.6 %multiply_reduce_fusion.1 = (f32[64,16,32]{0,2,1:T(8,128)S(1)}, f32[9,16,32]{2,1,0:T(8,128)S(1)}) fusion(f32[1,64,16,32]{1,3,2,0:T(8,128)S(1)} %bitcast.100, f32[3,64,16,32]{1,3,2,0:T(8,128)S(1)} %broadcast_in_dim.80, f32[5,64,16,32]{1,3,2,0:T(8,128)S(1)} %broadcast_in_dim.79, f32[9,64,16]{1,2,0:T(8,128)S(1)} %broadcast_multiply_fusion.1, ...), kind=kLoop, calls=%fused_computation.8 | loop fusion | flops 2321920 | bytes 1552384 | tf_op jit(solution)/shard_map/while/body/eval_jaxpr/transpose(jvp())/reduce_sum | solution.py:90
  47.5 3.1 %scatter_custom_fusion = f32[3,5184]{0,1:T(8,128)S(1)} fusion(s32[512]{0:T(512)S(1)} %bitcast.115, f32[512,3]{1,0:T(8,128)S(1)} %copy.179, f32[]{:T(128)} %constant.151.clone.1), kind=kCustom, calls=%fused_computation.13 | custom fusion | flops 1536 | bytes 62212 | tf_op jit(solution)/shard_map/while/body/eval_jaxpr/scatter-add | solution.py:207
  50.6 5.0 %scatter_fusion = f32[3,5184]{0,1:T(8,128)S(1)} fusion(f32[3,5184]{0,1:T(8,128)S(1)} %scatter_custom_fusion, s32[512]{0:T(512)S(1)} %bitcast.112, f32[512,3]{1,0:T(8,128)S(1)} %copy.180), kind=kCustom, calls=%fused_computation.3 | custom fusion | flops 1536 | bytes 20480 | tf_op jit(solution)/shard_map/while/body/eval_jaxpr/scatter-add | solution.py:208
  55.6 0.8 copy.181
  56.4 3.1 %reshape.353 = f32[3,12,12,12,3]{4,3,2,1,0:T(8,128)} reshape(f32[3,5184]{1,0:T(4,128)S(1)} %copy.181) | data formatting | bytes 124416 | tf_op jit(solution)/shard_map/reshape | solution.py:215
  59.5 1.4 %fusion.83 = (f32[2,12,12,3,3]{3,2,1,0,4:T(8,128)S(1)}, f32[2,12,12,3,3]{3,2,1,0,4:T(8,128)S(1)}) fusion(f32[12,12,12,3,3]{3,2,1,0,4:T(8,128)} %bitcast.92), kind=kLoop, calls=%fused_computation.199 | loop fusion | bytes 41472 | tf_op jit(solution)/shard_map/slice | solution.py:118
  60.9 0.6 copy.183
  61.4 0.6 collective-permute-start.6
  62.1 0.6 copy.184
  62.6 2.3 %collective-permute-start.7 = (f32[2,12,12,9]{2,0,3,1:T(2,128)S(1)}, f32[2,12,12,9]{2,0,3,1:T(2,128)S(1)}, u32[]{:S(2)}, u32[]{:S(2)}) collective-permute-start(f32[2,12,12,9]{2,0,3,1:T(2,128)S(1)} %bitcast.108), channel_id=1, source_target_pairs={{0,24},{8,0},{16,8},{24,16},{1,25},{9,1},{17,9},{25,17},{2,26},{10... | collective-permute-start | bytes 31112 | tf_op jit(solution)/shard_map/ppermute | solution.py:23
  65.0 1.9 %slice.163 = f32[8,12,12,3,3]{3,2,1,0,4:T(8,128)S(1)} slice(f32[12,12,12,3,3]{3,2,1,0,4:T(8,128)} %bitcast.93), slice={[2:10], [0:12], [0:12], [0:3], [0:3]} | slice | bytes 82944 | tf_op jit(solution)/shard_map/slice | solution.py:119
  66.8 1.8 %copy.182 = f32[8,12,12,3,3]{2,0,4,3,1:T(8,128)S(1)} copy(f32[8,12,12,3,3]{3,2,1,0,4:T(8,128)S(1)} %slice.163) | data formatting | bytes 82944 | tf_op jit(solution)/shard_map/slice | solution.py:119
  68.7 1.2 %collective-permute-done.7 = f32[2,12,12,9]{2,0,3,1:T(2,128)S(1)} collective-permute-done((f32[2,12,12,9]{2,0,3,1:T(2,128)S(1)}, f32[2,12,12,9]{2,0,3,1:T(2,128)S(1)}, u32[]{:S(2)}, u32[]{:S(2)}) %collective-permute-start.7) | collective-permute-done | bytes 10400 | tf_op jit(solution)/shard_map/ppermute | solution.py:23
  70.0 1.2 %collective-permute-start.8 = (f32[8,2,12,9]{2,0,3,1:T(8,128)S(1)}, f32[8,2,12,9]{2,0,3,1:T(8,128)S(1)}, u32[]{:S(2)}, u32[]{:S(2)}) collective-permute-start(f32[8,2,12,9]{2,0,3,1:T(8,128)S(1)} %get-tuple-element.70), channel_id=1, source_target_pairs={{0,2},{2,4},{4,6},{6,0},{1,3},{3,5},{5,7},{7,1},{8,10},{10,12},{12... | collective-permute-start | bytes 20744 | tf_op jit(solution)/shard_map/ppermute | solution.py:23
  71.2 2.7 %collective-permute-start.9 = (f32[8,2,12,9]{2,0,3,1:T(8,128)S(1)}, f32[8,2,12,9]{2,0,3,1:T(8,128)S(1)}, u32[]{:S(2)}, u32[]{:S(2)}) collective-permute-start(f32[8,2,12,9]{2,0,3,1:T(8,128)S(1)} %get-tuple-element.71), channel_id=1, source_target_pairs={{0,6},{2,0},{4,2},{6,4},{1,7},{3,1},{5,3},{7,5},{8,14},{10,8},{12,... | collective-permute-start | bytes 20744 | tf_op jit(solution)/shard_map/ppermute | solution.py:23
  73.9 2.4 %collective-permute-done.8 = f32[8,2,12,9]{2,0,3,1:T(8,128)S(1)} collective-permute-done((f32[8,2,12,9]{2,0,3,1:T(8,128)S(1)}, f32[8,2,12,9]{2,0,3,1:T(8,128)S(1)}, u32[]{:S(2)}, u32[]{:S(2)}) %collective-permute-start.8) | collective-permute-done | bytes 6944 | tf_op jit(solution)/shard_map/ppermute | solution.py:23
  76.6 0.5 collective-permute-start.11
  77.1 0.6 reduce_sum.176
  78.8 0.4 copy.185
  79.2 0.8 %reshape.354 = f32[1,1,4608]{2,1,0:T(1,128)} reshape(f32[8,8,8,9]{3,2,1,0:T(8,128)S(1)} %copy.185) | data formatting | bytes 36864 | tf_op jit(solution)/shard_map/reshape | solution.py:221
  (110 shorter events, 8.9 us)
Async XLA Ops:
  0.6 39.7 %copy-start = (f32[256,64]{0,1:T(8,128)S(1)}, f32[256,64]{0,1:T(8,128)}, u32[]{:S(2)}) copy-start(f32[256,64]{0,1:T(8,128)} %param.23) | copy-start | bytes 196612
  2.7 11.0 %collective-permute-start = (f32[2,8,8,12]{3,2,1,0:T(8,128)S(1)}, f32[2,8,8,12]{3,2,1,0:T(8,128)S(1)}, u32[]{:S(2)}, u32[]{:S(2)}) collective-permute-start(f32[2,8,8,12]{3,2,1,0:T(8,128)S(1)} %get-tuple-element.68), channel_id=1, source_target_pairs={{0,8},{8,16},{16,24},{24,0},{1,9},{9,17},{17,25},{25,1},{2,10},{10... | collective-permute-start | bytes 18440 | tf_op jit(solution)/shard_map/ppermute | solution.py:33
  5.7 8.0 %collective-permute-start.1 = (f32[2,8,8,12]{3,2,1,0:T(8,128)S(1)}, f32[2,8,8,12]{3,2,1,0:T(8,128)S(1)}, u32[]{:S(2)}, u32[]{:S(2)}) collective-permute-start(f32[2,8,8,12]{3,2,1,0:T(8,128)S(1)} %get-tuple-element.69), channel_id=1, source_target_pairs={{8,0},{16,8},{24,16},{0,24},{9,1},{17,9},{25,17},{1,25},{10,2},{18... | collective-permute-start | bytes 18440 | tf_op jit(solution)/shard_map/ppermute | solution.py:34
  10.4 3.2 %copy-start.4 = (s32[1,1,16]{2,1,0:T(1,128)S(1)}, s32[1,1,16]{2,1,0:T(1,128)}, u32[]{:S(2)}) copy-start(s32[1,1,16]{2,1,0:T(1,128)} %param.18) | copy-start | bytes 196
  13.8 7.7 %collective-permute-start.2 = (f32[12,2,8,12]{3,2,1,0:T(8,128)S(1)}, f32[12,2,8,12]{3,2,1,0:T(8,128)S(1)}, u32[]{:S(2)}, u32[]{:S(2)}) collective-permute-start(f32[12,2,8,12]{3,2,1,0:T(8,128)S(1)} %get-tuple-element.63), channel_id=1, source_target_pairs={{0,2},{2,4},{4,6},{6,0},{1,3},{3,5},{5,7},{7,1},{8,10},{10,12},{12... | collective-permute-start | bytes 27656 | tf_op jit(solution)/shard_map/ppermute | solution.py:33
  15.9 5.8 %collective-permute-start.3 = (f32[12,2,8,12]{3,2,1,0:T(8,128)S(1)}, f32[12,2,8,12]{3,2,1,0:T(8,128)S(1)}, u32[]{:S(2)}, u32[]{:S(2)}) collective-permute-start(f32[12,2,8,12]{3,2,1,0:T(8,128)S(1)} %get-tuple-element.64), channel_id=1, source_target_pairs={{2,0},{4,2},{6,4},{0,6},{3,1},{5,3},{7,5},{1,7},{10,8},{12,10},{14... | collective-permute-start | bytes 27656 | tf_op jit(solution)/shard_map/ppermute | solution.py:34
  21.9 4.0 %collective-permute-start.4 = (f32[12,12,2,12]{3,2,1,0:T(2,128)S(1)}, f32[12,12,2,12]{3,2,1,0:T(2,128)S(1)}, u32[]{:S(2)}, u32[]{:S(2)}) collective-permute-start(f32[12,12,2,12]{3,2,1,0:T(2,128)S(1)} %get-tuple-element.61), channel_id=1, source_target_pairs={{0,1},{1,0},{2,3},{3,2},{4,5},{5,4},{6,7},{7,6},{8,9},{9,8},{10,11... | collective-permute-start | bytes 41480 | tf_op jit(solution)/shard_map/ppermute | solution.py:33
  22.0 3.9 %collective-permute-start.5 = (f32[12,12,2,12]{3,2,1,0:T(2,128)S(1)}, f32[12,12,2,12]{3,2,1,0:T(2,128)S(1)}, u32[]{:S(2)}, u32[]{:S(2)}) collective-permute-start(f32[12,12,2,12]{3,2,1,0:T(2,128)S(1)} %get-tuple-element.62), channel_id=1, source_target_pairs={{1,0},{0,1},{3,2},{2,3},{5,4},{4,5},{7,6},{6,7},{9,8},{8,9},{11,10... | collective-permute-start | bytes 41480 | tf_op jit(solution)/shard_map/ppermute | solution.py:34
  26.3 1.4 %copy-start.1 = (f32[12,12,12,12]{3,2,1,0:T(8,128)}, f32[12,12,12,12]{3,2,1,0:T(8,128)S(1)}, u32[]{:S(2)}) copy-start(f32[12,12,12,12]{3,2,1,0:T(8,128)S(1)} %pad_maximum_fusion) | copy-start | bytes 248836
  32.3 3.7 %copy-start.3 = (f32[12,64]{1,0:T(8,128)S(1)}, f32[12,64]{1,0:T(8,128)}, u32[]{:S(2)}) copy-start(f32[12,64]{1,0:T(8,128)} %param.20) | copy-start | bytes 9220
  32.3 4.0 %copy-start.5 = (f32[64,64]{1,0:T(8,128)S(1)}, f32[64,64]{1,0:T(8,128)}, u32[]{:S(2)}) copy-start(f32[64,64]{1,0:T(8,128)} %param.21) | copy-start | bytes 49156
  32.5 4.3 %copy-start.2 = (f32[64,64]{1,0:T(8,128)S(1)}, f32[64,64]{1,0:T(8,128)}, u32[]{:S(2)}) copy-start(f32[64,64]{1,0:T(8,128)} %param.22) | copy-start | bytes 49156
  39.1 2.0 %copy-start.6 = (f32[64]{0:T(128)S(1)}, f32[64]{0:T(128)}, u32[]{:S(2)}) copy-start(f32[64]{0:T(128)} %param.24) | copy-start | bytes 772
  61.4 7.3 %collective-permute-start.6 = (f32[2,12,12,9]{2,0,3,1:T(2,128)S(1)}, f32[2,12,12,9]{2,0,3,1:T(2,128)S(1)}, u32[]{:S(2)}, u32[]{:S(2)}) collective-permute-start(f32[2,12,12,9]{2,0,3,1:T(2,128)S(1)} %bitcast.107), channel_id=1, source_target_pairs={{0,8},{8,16},{16,24},{24,0},{1,9},{9,17},{17,25},{25,1},{2,10},{10... | collective-permute-start | bytes 31112 | tf_op jit(solution)/shard_map/ppermute | solution.py:23
  62.6 7.2 %collective-permute-start.7 = (f32[2,12,12,9]{2,0,3,1:T(2,128)S(1)}, f32[2,12,12,9]{2,0,3,1:T(2,128)S(1)}, u32[]{:S(2)}, u32[]{:S(2)}) collective-permute-start(f32[2,12,12,9]{2,0,3,1:T(2,128)S(1)} %bitcast.108), channel_id=1, source_target_pairs={{0,24},{8,0},{16,8},{24,16},{1,25},{9,1},{17,9},{25,17},{2,26},{10... | collective-permute-start | bytes 31112 | tf_op jit(solution)/shard_map/ppermute | solution.py:23
  70.0 6.3 %collective-permute-start.8 = (f32[8,2,12,9]{2,0,3,1:T(8,128)S(1)}, f32[8,2,12,9]{2,0,3,1:T(8,128)S(1)}, u32[]{:S(2)}, u32[]{:S(2)}) collective-permute-start(f32[8,2,12,9]{2,0,3,1:T(8,128)S(1)} %get-tuple-element.70), channel_id=1, source_target_pairs={{0,2},{2,4},{4,6},{6,0},{1,3},{3,5},{5,7},{7,1},{8,10},{10,12},{12... | collective-permute-start | bytes 20744 | tf_op jit(solution)/shard_map/ppermute | solution.py:23
  71.2 5.2 %collective-permute-start.9 = (f32[8,2,12,9]{2,0,3,1:T(8,128)S(1)}, f32[8,2,12,9]{2,0,3,1:T(8,128)S(1)}, u32[]{:S(2)}, u32[]{:S(2)}) collective-permute-start(f32[8,2,12,9]{2,0,3,1:T(8,128)S(1)} %get-tuple-element.71), channel_id=1, source_target_pairs={{0,6},{2,0},{4,2},{6,4},{1,7},{3,1},{5,3},{7,5},{8,14},{10,8},{12,... | collective-permute-start | bytes 20744 | tf_op jit(solution)/shard_map/ppermute | solution.py:23
  76.5 1.6 %collective-permute-start.10 = (f32[8,8,2,9]{2,0,3,1:T(8,128)S(1)}, f32[8,8,2,9]{2,0,3,1:T(8,128)S(1)}, u32[]{:S(2)}, u32[]{:S(2)}) collective-permute-start(f32[8,8,2,9]{2,0,3,1:T(8,128)S(1)} %get-tuple-element.72), channel_id=1, source_target_pairs={{0,1},{1,0},{2,3},{3,2},{4,5},{5,4},{6,7},{7,6},{8,9},{9,8},{10,11... | collective-permute-start | bytes 13832 | tf_op jit(solution)/shard_map/ppermute | solution.py:23
  76.6 2.0 %collective-permute-start.11 = (f32[8,8,2,9]{2,0,3,1:T(8,128)S(1)}, f32[8,8,2,9]{2,0,3,1:T(8,128)S(1)}, u32[]{:S(2)}, u32[]{:S(2)}) collective-permute-start(f32[8,8,2,9]{2,0,3,1:T(8,128)S(1)} %get-tuple-element.73), channel_id=1, source_target_pairs={{0,1},{1,0},{2,3},{3,2},{4,5},{5,4},{6,7},{7,6},{8,9},{9,8},{10,11... | collective-permute-start | bytes 13832 | tf_op jit(solution)/shard_map/ppermute | solution.py:23
where the time goes:
time: 80.5 us; the launch traced here: 80.1 us
  local copies, waits for them, and re-layouts  28.1 us (35%)
  other arithmetic  22.2 us (28%)
  starting transfers between devices  16.2 us (20%)
  waiting for transfers between devices  8.1 us (10%)
  matrix products  3.46 us (4%)
  between operations  1.95 us (2%)
    ppermute x6, starting transfers between devices, shifted(): lax.ppermute(shard, axis, [(i, (i + by) % length) for i in range(length)])  7.43 us
    ppermute x3, starting transfers between devices, with_halo(): before = lax.ppermute(last, axis, up)  5.13 us
    scatter-add x1, other arithmetic, one_block(): forces = forces.at[:, first].add(grad)  5.01 us
    ppermute x6, waiting for transfers between devices, shifted(): lax.ppermute(shard, axis, [(i, (i + by) % length) for i in range(length)])  4.39 us
    slice x2, local copies, waits for them, and re-layouts, fold_layers(): inner = lax.slice_in_dim(values, 2, length - 2, axis=axis_dim)  3.69 us
    ppermute x3, starting transfers between devices, with_halo(): after = lax.ppermute(first, axis, down)  3.61 us
    ppermute x3, waiting for transfers between devices, with_halo(): before = lax.ppermute(last, axis, up)  3.54 us
    add x1, local copies, waits for them, and re-layouts, local(): corner[:, :, :, None, :] + sites[None, None, None, :, :] + shifts  3.33 us
  transfers between devices with their start and end apart: 12, of which 6 were waited for; matrix products, arithmetic and copies ran while one was open for 18% of the time, Pallas kernels for 0%

commit v1 on v0

v1 whole, which is shorter than its diff:
```python
import math

import jax
import jax.numpy as jnp
from jax import lax
from jax.experimental import pallas as pl
from jax.experimental.pallas import tpu as pltpu
from jax.sharding import PartitionSpec as P

CELLS = 8
NBASIS = 8
CUTOFF = 6.0
SIDE = 3.1
ENV = 0.2
LANES = 128
ZROWS = CELLS * 9
KINDS = CELLS * 3
AXES = ("gx", "gy", "gz")

NN = (((1,), (0,)), ((), ()))
NT = (((1,), (1,)), ((), ()))


def halves(x):
    hi = x.astype(jnp.bfloat16)
    lo = (x - hi.astype(jnp.float32)).astype(jnp.bfloat16)
    return hi, lo


def raw(a, b, dims):
    return lax.dot_general(a, b, dims, preferred_element_type=jnp.float32)


def mm(a, b, dims=NN):
    ah, al = a if isinstance(a, tuple) else halves(a)
    bh, bl = b if isinstance(b, tuple) else halves(b)
    return raw(ah, bh, dims) + (raw(ah, bl, dims) + raw(al, bh, dims))


def mm_exact_b(a, b, dims=NN):
    ah, al = halves(a)
    return raw(ah, b, dims) + raw(al, b, dims)


def mm_exact_a(a, b, dims=NN):
    bh, bl = halves(b)
    return raw(a, bh, dims) + raw(a, bl, dims)


def slot_plan(depth):
    plan = []
    tile = CELLS
    for dz in [0, 1] if depth == 2 else [0, 1, -1]:
        for dx in (-1, 0, 1):
            for dy in (-1, 0, 1):
                if dx == dy == dz == 0:
                    continue
                if dx == 0 and dy == 0:
                    tiles = CELLS
                elif dz == 0 and (dx == 0 or dy == 0):
                    tiles = 2
                else:
                    tiles = 1
                plan.append((dx, dy, dz, tile, tiles))
                tile += tiles
    return plan, tile


def origin(step, tiles):
    return 0 if step >= 0 else CELLS - tiles


def wave(turns):
    f = turns - jnp.floor(turns + 0.5)
    f = jnp.where(f > 0.25, 0.5 - f, jnp.where(f < -0.25, -0.5 - f, f))
    x = f * (2.0 * math.pi)
    s = x * x
    p = -1.0 / 39916800.0
    for c in (1.0 / 362880.0, -1.0 / 5040.0, 1.0 / 120.0, -1.0 / 6.0):
        p = p * s + c
    return x + x * s * p


def divided(value, by):
    return jnp.floor((value + 0.5) * (1.0 / by))


def silu_pair(x):
    s = 1.0 / (1.0 + jnp.exp(-x))
    return x * s, s * (1.0 + x * (1.0 - s))


def kernel_body(sizes, plan, disp, spec, cen, nbr, cnt, alive, w_two, w_lat, w_env, w_out,
                readout, energy, forces, table, pack, part, got, total,
                send_a, recv_a, send_b, recv_b):
    me = tuple(lax.axis_index(a) for a in AXES)

    def peer(step, sign):
        return tuple(
            lax.rem(i + (sign * d + n), n) if d else i for i, d, n in zip(me, step, sizes)
        )

    barrier = pltpu.get_barrier_semaphore()
    for slot in plan:
        pl.semaphore_signal(
            barrier, inc=1, device_id=peer(slot[:3], 1), device_id_type=pl.DeviceIdType.MESH
        )

    dline = jnp.concatenate([disp[pl.ds(k, 4, stride=9), :] for k in range(9)], axis=1)
    sline = jnp.concatenate([spec[pl.ds(k, 4, stride=3), :] for k in range(3)], axis=1)
    sline = sline.astype(jnp.float32)
    blank = jnp.zeros((4, LANES - ZROWS - KINDS), jnp.float32)
    for j in range(16):
        table[pl.ds(j, 4, stride=16), :] = jnp.concatenate(
            [
                dline[:, ZROWS * j : ZROWS * (j + 1)],
                sline[:, KINDS * j : KINDS * (j + 1)],
                blank,
            ],
            axis=1,
        )
    for t, y in enumerate((0, 1, CELLS - 2, CELLS - 1)):
        pack[pl.ds(8 * t, 8), :] = table[pl.ds(y, 8, stride=8), :]

    pl.semaphore_wait(barrier, len(plan))
    inward = []
    for at, (dx, dy, dz, tile, tiles) in enumerate(plan):
        if dx == 0 and dy != 0:
            first = 0 if dy > 0 else 4 - tiles
            source = pack.at[pl.ds(8 * first, 8 * tiles)]
        else:
            source = table.at[pl.ds(8 * origin(dx, tiles), 8 * tiles)]
        copy = pltpu.make_async_remote_copy(
            src_ref=source,
            dst_ref=table.at[pl.ds(8 * tile, 8 * tiles)],
            send_sem=send_a.at[at],
            recv_sem=recv_a.at[at],
            device_id=peer((dx, dy, dz), -1),
            device_id_type=pl.DeviceIdType.MESH,
        )
        copy.start()
        inward.append(copy)

    pairs = nbr.shape[1]
    centre_total = cen.shape[1]
    slots = pairs // centre_total
    lane = lax.broadcasted_iota(jnp.int32, (centre_total, pairs), 1)
    row = lax.broadcasted_iota(jnp.int32, (centre_total, pairs), 0)
    mine = ((lane >= row * slots) & (lane < (row + 1) * slots)).astype(jnp.float32)
    mine16 = mine.astype(jnp.bfloat16)
    lists = jnp.concatenate(
        [cen[...], cnt[...], jnp.zeros((6, centre_total), jnp.int32)], axis=0
    ).astype(jnp.float32)
    spread = mm_exact_b(lists, mine16)
    first, count = spread[0:1], spread[1:2]
    lane1 = lax.broadcasted_iota(jnp.int32, (1, pairs), 1)
    lanef = lane1.astype(jnp.float32)
    centre_id = divided(lanef, slots)
    slot_id = lanef - centre_id * slots
    live = jnp.where(
        (slot_id < count) & (lane1 < alive[0, 0] * slots), 1.0, 0.0
    ).astype(jnp.float32)

    cell_i = divided(first, 3.0)
    atom_i = first - 3.0 * cell_i
    col_i = divided(cell_i, CELLS)
    z_i = cell_i - CELLS * col_i
    x_i = divided(col_i, CELLS)
    y_i = col_i - CELLS * x_i

    second = nbr[...].astype(jnp.float32)
    ext = CELLS + 4
    cell_j = divided(second, 3.0)
    atom_j = second - 3.0 * cell_j
    col_j = divided(cell_j, ext)
    z_j = cell_j - ext * col_j - 2.0
    x_j = divided(col_j, ext)
    y_j = col_j - ext * x_j - 2.0
    x_j = x_j - 2.0

    def side(v):
        return jnp.where(v < 0.0, -1.0, jnp.where(v >= CELLS, 1.0, 0.0))

    sx, sy, sz = side(x_j), side(y_j), side(z_j)
    x_in, y_in, z_in = x_j - CELLS * sx, y_j - CELLS * sy, z_j - CELLS * sz
    if sizes[2] == 2:
        sz = jnp.abs(sz)
    code = sx * 9.0 + sy * 3.0 + sz
    across, along = x_in * CELLS + y_in, y_in * CELLS + x_in
    line = across
    for dx, dy, dz, tile, tiles in plan:
        if dx == 0 and dy != 0:
            value = along + float(8 * tile - 8 * origin(dy, tiles))
        else:
            value = across + float(8 * tile - 8 * origin(dx, tiles))
        line = jnp.where(code == float(dx * 9 + dy * 3 + dz), value, line)

    rows = table.shape[0]
    own = CELLS * CELLS

    def hot(index, length):
        ids = lax.broadcasted_iota(jnp.int32, (length, pairs), 0)
        return jnp.where(ids == index.astype(jnp.int32), 1.0, 0.0).astype(jnp.bfloat16)

    hot_j, hot_i = hot(line, rows), hot(col_i, own)
    lanes72 = lax.broadcasted_iota(jnp.int32, (ZROWS, pairs), 0)
    lanes24 = lax.broadcasted_iota(jnp.int32, (KINDS, pairs), 0)

    def site(atom):
        one, two = atom == 1.0, atom == 2.0
        return (
            jnp.where(one, 0.75, 0.25),
            jnp.where(one | two, 0.75, 0.25),
            jnp.where(two, 0.75, 0.25),
        )

    def picked(stack, place):
        at = place.astype(jnp.int32)
        body = stack[0:ZROWS]
        out = [
            jnp.sum(jnp.where(lanes72 == 3 * at + c, body, 0.0), axis=0, keepdims=True)
            for c in range(3)
        ]
        kind = jnp.sum(
            jnp.where(lanes24 == at, stack[ZROWS : ZROWS + KINDS], 0.0), axis=0, keepdims=True
        )
        return out, kind

    def fetch(block, onehot):
        hi, lo = halves(block.T)
        return raw(hi, onehot, NN) + raw(lo, onehot, NN)

    place_i, place_j = z_i * 3.0 + atom_i, z_in * 3.0 + atom_j
    shift_i, kind_i = picked(fetch(table[pl.ds(0, own), :], hot_i), place_i)
    site_i, site_j = site(atom_i), site(atom_j)
    two = w_two[...]
    two = jnp.concatenate([two[4:12], two[0:4], jnp.zeros_like(two[0:4])], axis=0)
    two_t, lat_t, env_t, out_t = two.T, w_lat[...].T, w_env[...].T, w_out[...].T

    for copy in inward:
        copy.wait()

    shift_j, kind_j = picked(fetch(table[...], hot_j), place_j)
    rx, ry, rz = [
        ((b - a) + (tb - ta) + (sb - sa)) * SIDE
        for a, b, ta, tb, sa, sb in zip(
            (x_i, y_i, z_i), (x_j, y_j, z_j), site_i, site_j, shift_i, shift_j
        )
    ]
    dist = jnp.sqrt(rx * rx + ry * ry + rz * rz)
    inv = 1.0 / dist
    ux, uy, uz = rx * inv, ry * inv, rz * inv
    ratio = dist * (1.0 / CUTOFF)
    r2 = ratio * ratio
    r5 = r2 * r2 * ratio
    inside = ratio < 1.0
    bell = jnp.where(inside, 1.0 + r5 * ratio * (-28.0 + ratio * (48.0 - 21.0 * ratio)), 0.0)
    slope = jnp.where(
        inside, r5 * (1.0 - ratio) * (1.0 - ratio) * (-168.0 / CUTOFF), 0.0
    )
    order = (lax.broadcasted_iota(jnp.int32, (NBASIS, pairs), 0) + 1).astype(jnp.float32)
    turns = order * (dist * (0.5 / CUTOFF))
    sines, cosines = wave(turns), wave(turns + 0.25)
    norm = math.sqrt(2.0 / CUTOFF)
    basis = norm * sines * (inv * bell)
    basis_d = norm * (
        cosines * order * (inv * bell * (math.pi / CUTOFF))
        + sines * (inv * (slope - bell * inv))
    )
    kinds = [1.0 - kind_i, kind_i, 1.0 - kind_j, kind_j]
    inputs = jnp.concatenate([basis] + kinds + [jnp.zeros((4, pairs), jnp.float32)], axis=0)

    hidden, hidden_d = silu_pair(mm(two_t, inputs))
    latent, latent_d = silu_pair(mm(lat_t, hidden))
    latent_h = halves(latent)
    plain = mm(env_t, latent_h)
    scale = bell * live
    weight = plain * scale
    s3, s5, s15 = math.sqrt(3.0), math.sqrt(5.0), math.sqrt(15.0)
    harm = [
        jnp.ones_like(ux),
        s3 * ux,
        s3 * uy,
        s3 * uz,
        s15 * ux * uy,
        s15 * uy * uz,
        0.5 * s5 * (3.0 * uz * uz - 1.0),
        s15 * ux * uz,
        0.5 * s15 * (ux * ux - uy * uy),
    ]
    spread_y = halves(jnp.concatenate([h * mine for h in harm], axis=0))
    weight_h = halves(weight)
    bounds = [(0, 1), (1, 4), (4, 9)]
    cuts = [slice(a * centre_total, b * centre_total) for a, b in bounds]

    def cut(pair, s):
        return pair[0][s], pair[1][s]

    environ = ENV * mm(spread_y, weight_h, NT)
    mixed = [mm(environ[s].T, cut(spread_y, s)) for s in cuts]
    width = latent.shape[0]
    joined = jnp.concatenate([latent] + [weight * a for a in mixed], axis=0)
    updated, updated_d = silu_pair(mm(out_t, joined))
    column = jnp.broadcast_to(readout[...], (8, width)).T[:, 0:1]
    score = jnp.sum(column * updated, axis=0, keepdims=True)
    pair_energy = score * scale
    energy[...] = mm_exact_b(jnp.broadcast_to(pair_energy, (8, pairs)), mine16, NT)[0:1]

    d_out = (column * scale) * updated_d
    back = mm(w_out[...], d_out)
    d_mixed = [back[width * (k + 1) : width * (k + 2)] for k in range(3)]
    d_weight = d_mixed[0] * mixed[0] + d_mixed[1] * mixed[1] + d_mixed[2] * mixed[2]
    passing = [halves(q * weight) for q in d_mixed]
    d_environ = ENV * jnp.concatenate(
        [mm(cut(spread_y, s), p, NT) for s, p in zip(cuts, passing)], axis=0
    )
    d_weight = d_weight + mm(d_environ.T, spread_y)
    d_spread = jnp.concatenate(
        [mm(environ[s], p) for s, p in zip(cuts, passing)], axis=0
    ) + mm(d_environ, weight_h)
    d_harm = [
        jnp.sum(
            d_spread[m * centre_total : (m + 1) * centre_total] * mine, axis=0, keepdims=True
        )
        for m in range(9)
    ]
    d_scale = score + jnp.sum(d_weight * plain, axis=0, keepdims=True)
    d_latent = back[0:width] + mm(w_env[...], d_weight * scale)
    d_hidden = mm(w_lat[...], d_latent * latent_d)
    d_inputs = mm(two, d_hidden * hidden_d)
    d_dist = (
        jnp.sum(d_inputs[0:NBASIS] * basis_d, axis=0, keepdims=True) + d_scale * live * slope
    )
    dux = s3 * d_harm[1] + s15 * (uy * d_harm[4] + uz * d_harm[7] + ux * d_harm[8])
    duy = s3 * d_harm[2] + s15 * (ux * d_harm[4] + uz * d_harm[5] - uy * d_harm[8])
    duz = s3 * d_harm[3] + s15 * (uy * d_harm[5] + ux * d_harm[7]) + 3.0 * s5 * uz * d_harm[6]
    radial = d_dist - (ux * dux + uy * duy + uz * duz) * inv
    grad = [d * inv + u * radial for d, u in ((dux, ux), (duy, uy), (duz, uz))]

    def placed(place, sign):
        at = 3 * place.astype(jnp.int32)
        out = jnp.zeros((ZROWS, pairs), jnp.float32)
        for c in range(3):
            out = jnp.where(lanes72 == at + c, sign * grad[c], out)
        return jnp.concatenate(
            [out, jnp.zeros((LANES - ZROWS, pairs), jnp.float32)], axis=0
        )

    part[...] = mm_exact_a(hot_j, placed(place_j, -1.0), NT)
    outward = []
    for at, (dx, dy, dz, tile, tiles) in enumerate(plan):
        copy = pltpu.make_async_remote_copy(
            src_ref=part.at[pl.ds(8 * tile, 8 * tiles)],
            dst_ref=got.at[pl.ds(8 * tile, 8 * tiles)],
            send_sem=send_b.at[at],
            recv_sem=recv_b.at[at],
            device_id=peer((dx, dy, dz), 1),
            device_id_type=pl.DeviceIdType.MESH,
        )
        copy.start()
        outward.append(copy)
    total[...] = part[pl.ds(0, own), :] + mm_exact_a(hot_i, placed(place_i, 1.0), NT)
    for copy in outward:
        copy.wait()
    for dx, dy, dz, tile, tiles in plan:
        if dx == 0 and dy != 0:
            for t in range(tiles):
                spot = pl.ds(origin(dy, tiles) + t, 8, stride=8)
                total[spot, :] = total[spot, :] + got[pl.ds(8 * (tile + t), 8), :]
        else:
            spot = pl.ds(8 * origin(dx, tiles), 8 * tiles)
            total[spot, :] = total[spot, :] + got[pl.ds(8 * tile, 8 * tiles), :]
    final = jnp.concatenate(
        [total[pl.ds(j, 4, stride=16), :][:, 0:ZROWS] for j in range(16)], axis=1
    )
    for k in range(9):
        forces[pl.ds(k, 4, stride=9), :] = final[:, LANES * k : LANES * (k + 1)]


def solution(mesh):
    sizes = tuple(mesh.shape[a] for a in AXES)
    plan, tile_total = slot_plan(sizes[2])

    def local(displacement, species, centres, neighbours, neighbour_count, live_centres,
              w_two, w_lat, w_env, w_out, readout):
        centre_total = centres.shape[2]
        atoms = displacement.shape[2]
        vmem = pl.BlockSpec(memory_space=pltpu.VMEM)
        rows = 8 * tile_total

        def body(*refs):
            kernel_body(sizes, plan, *refs)

        energy, forces = pl.pallas_call(
            body,
            out_shape=(
                jax.ShapeDtypeStruct((1, centre_total), jnp.float32),
                jax.ShapeDtypeStruct((atoms // LANES, LANES), jnp.float32),
            ),
            in_specs=[vmem] * 5
            + [pl.BlockSpec(memory_space=pltpu.SMEM)]
            + [vmem] * 5,
            out_specs=(vmem, vmem),
            scratch_shapes=[
                pltpu.VMEM((rows, LANES), jnp.float32),
                pltpu.VMEM((32, LANES), jnp.float32),
                pltpu.VMEM((rows, LANES), jnp.float32),
                pltpu.VMEM((rows, LANES), jnp.float32),
                pltpu.VMEM((CELLS * CELLS, LANES), jnp.float32),
            ]
            + [pltpu.SemaphoreType.DMA((len(plan),))] * 4,
            compiler_params=pltpu.CompilerParams(collective_id=0, has_side_effects=True),
        )(
            displacement.reshape(-1, LANES),
            species.reshape(-1, LANES),
            centres.reshape(1, -1),
            neighbours.reshape(1, -1),
            neighbour_count.reshape(1, -1),
            live_centres.reshape(1, 1),
            w_two, w_lat, w_env, w_out, readout.reshape(1, -1),
        )
        return energy.reshape(1, 1, -1), forces.reshape(1, 1, -1)

    split = P(*AXES)
    return jax.shard_map(
        local,
        mesh=mesh,
        in_specs=(split,) * 6 + (P(),) * 5,
        out_specs=(split, split),
        check_vma=False,
    )
```

time: 80.5 us -> 30.4 us (0.38)
  local copies, waits for them, and re-layouts: 28.1 us -> 2.61 us
  Pallas kernels: 0 us -> 23.4 us
  other arithmetic: 22.2 us -> 2.68 us
  starting transfers between devices: 16.2 us -> 0 us
  waiting for transfers between devices: 8.1 us -> 0 us
  matrix products: 3.46 us -> 0 us
    pallas_call x0 -> x1, Pallas kernels: none -> 23.4 us  [local(): pl.pallas_call(body, out_shape=(jax.ShapeDtypeStruct((1, centre_total), j...]
    ppermute x12 -> x0, starting transfers between devices: 16.2 us -> none  [the longest x6 7.43 us: shifted(): lax.ppermute(shard, axis, [(i, (i + by) % length) for i in range(length)])]
    reshape x10 -> x1, local copies, waits for them, and re-layouts: 9.53 us -> 1.35 us  [local(): return (energy.reshape(1, 1, -1), forces.reshape(1, 1, -1))]
    scatter-add x2 -> x0, other arithmetic: 8.13 us -> none  [the longest x1 5.01 us: one_block(): forces = forces.at[:, first].add(grad)]
    ppermute x12 -> x0, waiting for transfers between devices: 8.1 us -> none  [the longest x6 4.39 us: shifted(): lax.ppermute(shard, axis, [(i, (i + by) % length) for i in range(length)])]
    slice x11 -> x0, local copies, waits for them, and re-layouts: 7.78 us -> none  [the longest x2 3.69 us: fold_layers(): inner = lax.slice_in_dim(values, 2, length - 2, axis=axis_dim)]
    reduce_sum x10 -> x0, other arithmetic: 4.43 us -> none  [the longest x1 1.56 us: block_energy(): harm[:, None, :] * weights[None, :, :]]
    add x5 -> x0, other arithmetic: 4.02 us -> none  [the longest x1 2.97 us: local(): corner[:, :, :, None, :] + sites[None, None, None, :, :] + shifts]
  transfers between devices with their start and end apart: 12 -> 0, of which waited for: 6 -> 0; matrix products, arithmetic and copies ran while one was open for 18% -> 0% of each run, Pallas kernels for 0% -> 0%
where the time goes in v1:
time: 30.4 us; the launch traced here: 30 us
  Pallas kernels  23.4 us (77%)
  other arithmetic  2.68 us (9%)
  local copies, waits for them, and re-layouts  2.61 us (9%)
  between operations  1.33 us (4%)
    pallas_call x1, Pallas kernels, local(): pl.pallas_call(body, out_shape=(jax.ShapeDtypeStruct((1, centre_total), j...  23.4 us
    unnamed x2, other arithmetic  2.68 us
    reshape x1, local copies, waits for them, and re-layouts, local(): return (energy.reshape(1, 1, -1), forces.reshape(1, 1, -1))  1.35 us
    unnamed x6, local copies, waits for them, and re-layouts  1.26 us

profile of v1, /device:TPU:0, one launch (start us, length us, event | category | flops | bytes accessed | tf_op | source)
XLA Modules:
  0.0 30.0 jit_solution(13255925580864098463)
XLA Ops:
  0.6 0.0 copy-start
  1.3 1.3 %reduce.1 = s32[1536]{0:T(1024)} reduce(s32[1,1,1536]{2,1,0:T(1,128)} %param.12, s32[]{:T(128)} %constant.7), dimensions={0,1}, to_apply=%param.12.reduce_sub_computation | reduce | bytes 12292 | tf_op args[1]
  2.6 1.4 %reduce = f32[4608]{0:T(1024)} reduce(f32[1,1,4608]{2,1,0:T(1,128)} %param.11, f32[]{:T(128)} %constant.6), dimensions={0,1}, to_apply=%param.11.reduce_sub_computation | reduce | bytes 36868 | tf_op args[0]
  4.0 0.0 copy-done
  4.0 0.7 %copy.13.refs_9_ = f32[256,64]{1,0:T(8,128)} copy(f32[256,64]{0,1:T(8,128)S(1)} %copy-done) | data formatting | bytes 131072 | tf_op args[9]
  4.7 23.4 %shard_map.122 = (f32[1,16]{1,0:T(1,128)}, f32[36,128]{1,0:T(8,128)}) custom-call(f32[36,128]{1,0:T(8,128)} %bitcast.9, s32[12,128]{1,0:T(8,128)} %bitcast.10, s32[1,16]{1,0:T(1,128)} %bitcast.12, s32[1,512]{1,0:T(1,128)} %bitcast.11, s32[1,16]{1,0:T(1,128)} %bitcast.13, s32[1,1]{1,0:T(1,128)} %bitcast.8.refs_5_, f32[12,64]{1,0:T(8,128)} %refs_6_.1, ...), custom_call_target="tpu_custom_call" | custom-call | tf_op jit(solution)/shard_map/pallas_call | solution.py:394
  28.2 0.0 copy-start.1
  28.2 1.4 %reshape.39 = f32[1,1,4608]{2,1,0:T(1,128)} reshape(f32[36,128]{1,0:T(8,128)} %get-tuple-element.5) | data formatting | bytes 36864 | tf_op jit(solution)/shard_map/reshape | solution.py:422
  29.5 0.0 copy-done.1
  29.5 0.5 %copy.16 = f32[1,1,16]{2,1,0:T(1,128)} copy(f32[1,1,16]{2,1,0:T(1,128)S(1)} %bitcast.15) | data formatting | bytes 128
Async XLA Ops:
  0.6 3.4 %copy-start = (f32[256,64]{0,1:T(8,128)S(1)}, f32[256,64]{0,1:T(8,128)}, u32[]{:S(2)}) copy-start(f32[256,64]{0,1:T(8,128)} %param.20) | copy-start | bytes 196612
  28.2 1.4 %copy-start.1 = (f32[1,16]{1,0:T(1,128)S(1)}, f32[1,16]{1,0:T(1,128)}, u32[]{:S(2)}) copy-start(f32[1,16]{1,0:T(1,128)} %get-tuple-element.4) | copy-start | bytes 196

commit v2 on v1

--- a/solution.py
+++ b/solution.py
@@ -90,9 +90,33 @@
     return x * s, s * (1.0 + x * (1.0 - s))
 
 
-def kernel_body(sizes, plan, disp, spec, cen, nbr, cnt, alive, w_two, w_lat, w_env, w_out,
-                readout, energy, forces, table, pack, part, got, total,
-                send_a, recv_a, send_b, recv_b):
+def kernel_body(sizes, plan, disp_hbm, spec_hbm, cen_hbm, nbr_hbm, cnt_hbm, alive_hbm, two_hbm,
+                lat_hbm, env_hbm, out_hbm, readout_hbm, energy, forces,
+                disp, spec, cen, nbr, cnt, alive, w_two, w_lat, w_env, w_out_t, readout,
+                table, pack, part, got, total, send_a, recv_a, send_b, recv_b, load):
+    loads = [
+        pltpu.make_async_copy(src, dst, load.at[at])
+        for at, (src, dst) in enumerate(
+            (
+                (disp_hbm, disp),
+                (spec_hbm, spec),
+                (cen_hbm, cen),
+                (nbr_hbm, nbr),
+                (cnt_hbm, cnt),
+                (alive_hbm, alive),
+                (two_hbm, w_two),
+                (lat_hbm, w_lat),
+                (env_hbm, w_env),
+                (out_hbm, w_out_t),
+                (readout_hbm, readout),
+            )
+        )
+    ]
+    for copy in loads:
+        copy.start()
+    disp, spec, cen, nbr, cnt, alive, energy, forces = (
+        ref.at[0] for ref in (disp, spec, cen, nbr, cnt, alive, energy, forces)
+    )
     me = tuple(lax.axis_index(a) for a in AXES)
 
     def peer(step, sign):
@@ -106,8 +130,11 @@
             barrier, inc=1, device_id=peer(slot[:3], 1), device_id_type=pl.DeviceIdType.MESH
         )
 
-    dline = jnp.concatenate([disp[pl.ds(k, 4, stride=9), :] for k in range(9)], axis=1)
-    sline = jnp.concatenate([spec[pl.ds(k, 4, stride=3), :] for k in range(3)], axis=1)
+    for copy in loads[:2]:
+        copy.wait()
+    dwide, swide = 16 * ZROWS, 16 * KINDS
+    dline = jnp.concatenate([disp[:, dwide * q : dwide * (q + 1)] for q in range(4)], axis=0)
+    sline = jnp.concatenate([spec[:, swide * q : swide * (q + 1)] for q in range(4)], axis=0)
     sline = sline.astype(jnp.float32)
     blank = jnp.zeros((4, LANES - ZROWS - KINDS), jnp.float32)
     for j in range(16):
@@ -123,8 +150,7 @@
         pack[pl.ds(8 * t, 8), :] = table[pl.ds(y, 8, stride=8), :]
 
     pl.semaphore_wait(barrier, len(plan))
-    inward = []
-    for at, (dx, dy, dz, tile, tiles) in enumerate(plan):
+    for dx, dy, dz, tile, tiles in plan:
         if dx == 0 and dy != 0:
             first = 0 if dy > 0 else 4 - tiles
             source = pack.at[pl.ds(8 * first, 8 * tiles)]
@@ -133,13 +159,15 @@
         copy = pltpu.make_async_remote_copy(
             src_ref=source,
             dst_ref=table.at[pl.ds(8 * tile, 8 * tiles)],
-            send_sem=send_a.at[at],
-            recv_sem=recv_a.at[at],
+            send_sem=send_a.at[0],
+            recv_sem=recv_a.at[0],
             device_id=peer((dx, dy, dz), -1),
             device_id_type=pl.DeviceIdType.MESH,
         )
         copy.start()
-        inward.append(copy)
+
+    for copy in loads[2:]:
+        copy.wait()
 
     pairs = nbr.shape[1]
     centre_total = cen.shape[1]
@@ -158,7 +186,7 @@
     centre_id = divided(lanef, slots)
     slot_id = lanef - centre_id * slots
     live = jnp.where(
-        (slot_id < count) & (lane1 < alive[0, 0] * slots), 1.0, 0.0
+        (slot_id < count) & (lane1 < alive[...] * slots), 1.0, 0.0
     ).astype(jnp.float32)
 
     cell_i = divided(first, 3.0)
@@ -235,10 +263,22 @@
     site_i, site_j = site(atom_i), site(atom_j)
     two = w_two[...]
     two = jnp.concatenate([two[4:12], two[0:4], jnp.zeros_like(two[0:4])], axis=0)
-    two_t, lat_t, env_t, out_t = two.T, w_lat[...].T, w_env[...].T, w_out[...].T
-
-    for copy in inward:
-        copy.wait()
+    two_t, lat_t, env_t, out_t = two.T, w_lat[...].T, w_env[...].T, w_out_t[...]
+
+    arrived = pl.ds(own, rows - own)
+
+    def settle(ref, send, recv):
+        every = pltpu.make_async_remote_copy(
+            src_ref=ref.at[arrived],
+            dst_ref=ref.at[arrived],
+            send_sem=send.at[0],
+            recv_sem=recv.at[0],
+            device_id=peer(plan[0][:3], 1),
+            device_id_type=pl.DeviceIdType.MESH,
+        )
+        every.wait()
+
+    settle(table, send_a, recv_a)
 
     shift_j, kind_j = picked(fetch(table[...], hot_j), place_j)
     rx, ry, rz = [
@@ -307,7 +347,7 @@
     energy[...] = mm_exact_b(jnp.broadcast_to(pair_energy, (8, pairs)), mine16, NT)[0:1]
 
     d_out = (column * scale) * updated_d
-    back = mm(w_out[...], d_out)
+    back = mm(out_t.T, d_out)
     d_mixed = [back[width * (k + 1) : width * (k + 2)] for k in range(3)]
     d_weight = d_mixed[0] * mixed[0] + d_mixed[1] * mixed[1] + d_mixed[2] * mixed[2]
     passing = [halves(q * weight) for q in d_mixed]
@@ -347,21 +387,18 @@
         )
 
     part[...] = mm_exact_a(hot_j, placed(place_j, -1.0), NT)
-    outward = []
-    for at, (dx, dy, dz, tile, tiles) in enumerate(plan):
+    for dx, dy, dz, tile, tiles in plan:
         copy = pltpu.make_async_remote_copy(
             src_ref=part.at[pl.ds(8 * tile, 8 * tiles)],
             dst_ref=got.at[pl.ds(8 * tile, 8 * tiles)],
-            send_sem=send_b.at[at],
-            recv_sem=recv_b.at[at],
+            send_sem=send_b.at[0],
+            recv_sem=recv_b.at[0],
             device_id=peer((dx, dy, dz), 1),
             device_id_type=pl.DeviceIdType.MESH,
         )
         copy.start()
-        outward.append(copy)
     total[...] = part[pl.ds(0, own), :] + mm_exact_a(hot_i, placed(place_i, 1.0), NT)
-    for copy in outward:
-        copy.wait()
+    settle(got, send_b, recv_b)
     for dx, dy, dz, tile, tiles in plan:
         if dx == 0 and dy != 0:
             for t in range(tiles):
@@ -373,8 +410,8 @@
     final = jnp.concatenate(
         [total[pl.ds(j, 4, stride=16), :][:, 0:ZROWS] for j in range(16)], axis=1
     )
-    for k in range(9):
-        forces[pl.ds(k, 4, stride=9), :] = final[:, LANES * k : LANES * (k + 1)]
+    for q in range(4):
+        forces[:, dwide * q : dwide * (q + 1)] = final[q : q + 1, :]
 
 
 def solution(mesh):
@@ -387,39 +424,34 @@
         atoms = displacement.shape[2]
         vmem = pl.BlockSpec(memory_space=pltpu.VMEM)
         rows = 8 * tile_total
+        args = [
+            displacement, species, centres, neighbours, neighbour_count, live_centres,
+            w_two, w_lat, w_env, w_out.T, readout.reshape(1, -1),
+        ]
 
         def body(*refs):
             kernel_body(sizes, plan, *refs)
 
-        energy, forces = pl.pallas_call(
+        return pl.pallas_call(
             body,
             out_shape=(
-                jax.ShapeDtypeStruct((1, centre_total), jnp.float32),
-                jax.ShapeDtypeStruct((atoms // LANES, LANES), jnp.float32),
+                jax.ShapeDtypeStruct(centres.shape, jnp.float32),
+                jax.ShapeDtypeStruct(displacement.shape, jnp.float32),
             ),
-            in_specs=[vmem] * 5
-            + [pl.BlockSpec(memory_space=pltpu.SMEM)]
-            + [vmem] * 5,
+            in_specs=[pl.BlockSpec(memory_space=pltpu.HBM)] * len(args),
             out_specs=(vmem, vmem),
-            scratch_shapes=[
+            scratch_shapes=[pltpu.VMEM(x.shape, x.dtype) for x in args]
+            + [
                 pltpu.VMEM((rows, LANES), jnp.float32),
                 pltpu.VMEM((32, LANES), jnp.float32),
                 pltpu.VMEM((rows, LANES), jnp.float32),
                 pltpu.VMEM((rows, LANES), jnp.float32),
                 pltpu.VMEM((CELLS * CELLS, LANES), jnp.float32),
             ]
-            + [pltpu.SemaphoreType.DMA((len(plan),))] * 4,
+            + [pltpu.SemaphoreType.DMA((1,))] * 4
+            + [pltpu.SemaphoreType.DMA((len(args),))],
             compiler_params=pltpu.CompilerParams(collective_id=0, has_side_effects=True),
-        )(
-            displacement.reshape(-1, LANES),
-            species.reshape(-1, LANES),
-            centres.reshape(1, -1),
-            neighbours.reshape(1, -1),
-            neighbour_count.reshape(1, -1),
-            live_centres.reshape(1, 1),
-            w_two, w_lat, w_env, w_out, readout.reshape(1, -1),
-        )
-        return energy.reshape(1, 1, -1), forces.reshape(1, 1, -1)
+        )(*args)
 
     split = P(*AXES)
     return jax.shard_map(

time: 30.4 us -> 26.1 us (0.86)
  other arithmetic: 2.68 us -> 0 us
  Pallas kernels: 23.4 us -> 22.1 us
    unnamed x2 -> x0, other arithmetic: 2.68 us -> none
    pallas_call x1, Pallas kernels: 23.4 us -> 22.1 us  [local(): pl.pallas_call(body, out_shape=(jax.ShapeDtypeStruct(centres.shape, jnp.f...]
    reshape x1 -> x0, local copies, waits for them, and re-layouts: 1.35 us -> none  [local(): return (energy.reshape(1, 1, -1), forces.reshape(1, 1, -1))]
    unnamed x6 -> x4, local copies, waits for them, and re-layouts: 1.26 us -> 2.47 us
where the time goes in v2:
time: 26.1 us; the launch traced here: 25.8 us
  Pallas kernels  22.1 us (85%)
  local copies, waits for them, and re-layouts  2.47 us (9%)
  between operations  1.3 us (5%)
    pallas_call x1, Pallas kernels, local(): pl.pallas_call(body, out_shape=(jax.ShapeDtypeStruct(centres.shape, jnp.f...  22.1 us
    unnamed x4, local copies, waits for them, and re-layouts  2.47 us

profile of v2, /device:TPU:0, one launch (start us, length us, event | category | flops | bytes accessed | tf_op | source)
XLA Modules:
  0.0 25.8 jit_solution(13421446942066287354)
XLA Ops:
  1.3 22.1 %shard_map.122 = (f32[1,1,16]{2,1,0:T(1,128)}, f32[1,1,4608]{2,1,0:T(1,128)}) custom-call(f32[1,1,4608]{2,1,0:T(1,128)} %refs_0_.1, s32[1,1,1536]{2,1,0:T(1,128)} %refs_1_.1, s32[1,1,16]{2,1,0:T(1,128)} %refs_2_.1, s32[1,1,512]{2,1,0:T(1,128)} %refs_3_.1, s32[1,1,16]{2,1,0:T(1,128)} %refs_4_.1, s32[1,1,1]{2,1,0:T(1,128)S(6)} %copy.15.refs_5_, ...), custom_call_target="tpu_custom_call" | custom-call | tf_op jit(solution)/shard_map/pallas_call | solution.py:435
  23.3 0.0 copy-start
  23.4 0.6 %copy-done = f32[1,1,16]{2,1,0:T(1,128)S(1)} copy-done((f32[1,1,16]{2,1,0:T(1,128)S(1)}, f32[1,1,16]{2,1,0:T(1,128)}, u32[]{:S(2)}) %copy-start) | copy-done | bytes 88
  24.0 0.5 %copy.16 = f32[1,1,16]{2,1,0:T(1,128)} copy(f32[1,1,16]{2,1,0:T(1,128)S(1)} %copy-done) | data formatting | bytes 128
  24.5 1.3 %copy.17 = f32[1,1,4608]{2,1,0:T(1,128)} copy(f32[1,1,4608]{2,1,0:T(1,128)} %get-tuple-element.5) | data formatting | bytes 36864
Async XLA Ops:
  23.3 0.6 %copy-start = (f32[1,1,16]{2,1,0:T(1,128)S(1)}, f32[1,1,16]{2,1,0:T(1,128)}, u32[]{:S(2)}) copy-start(f32[1,1,16]{2,1,0:T(1,128)} %get-tuple-element.4) | copy-start | bytes 196

commit v3 on v2

--- a/solution.py
+++ b/solution.py
@@ -34,7 +34,15 @@
 def mm(a, b, dims=NN):
     ah, al = a if isinstance(a, tuple) else halves(a)
     bh, bl = b if isinstance(b, tuple) else halves(b)
-    return raw(ah, bh, dims) + (raw(ah, bl, dims) + raw(al, bh, dims))
+    if dims is NT:
+        m, n = ah.shape[0], bh.shape[0]
+        both = raw(jnp.concatenate([ah, al], axis=0), jnp.concatenate([bh, bl], axis=0), NT)
+        return both[:m, :n] + (both[:m, n:] + both[m:, :n])
+    if ah.shape[1] > 2 * LANES - 1:
+        return raw(ah, bh, dims) + (raw(ah, bl, dims) + raw(al, bh, dims))
+    return raw(
+        jnp.concatenate([ah, ah, al], axis=1), jnp.concatenate([bh, bl, bh], axis=0), NN
+    )
 
 
 def mm_exact_b(a, b, dims=NN):
@@ -42,9 +50,10 @@
     return raw(ah, b, dims) + raw(al, b, dims)
 
 
-def mm_exact_a(a, b, dims=NN):
-    bh, bl = halves(b)
-    return raw(a, bh, dims) + raw(a, bl, dims)
+def mm_exact_a(a, b):
+    n = b.shape[0]
+    both = raw(a, jnp.concatenate(halves(b), axis=0), NT)
+    return both[:, :n] + both[:, n:]
 
 
 def slot_plan(depth):
@@ -91,9 +100,9 @@
 
 
 def kernel_body(sizes, plan, disp_hbm, spec_hbm, cen_hbm, nbr_hbm, cnt_hbm, alive_hbm, two_hbm,
-                lat_hbm, env_hbm, out_hbm, readout_hbm, energy, forces,
+                lat_hbm, env_hbm, out_hbm, readout_hbm, result,
                 disp, spec, cen, nbr, cnt, alive, w_two, w_lat, w_env, w_out_t, readout,
-                table, pack, part, got, total, send_a, recv_a, send_b, recv_b, load):
+                table, pack, part, got, send_a, recv_a, send_b, recv_b, load):
     loads = [
         pltpu.make_async_copy(src, dst, load.at[at])
         for at, (src, dst) in enumerate(
@@ -114,9 +123,10 @@
     ]
     for copy in loads:
         copy.start()
-    disp, spec, cen, nbr, cnt, alive, energy, forces = (
-        ref.at[0] for ref in (disp, spec, cen, nbr, cnt, alive, energy, forces)
-    )
+    disp, spec, cen, nbr, cnt, alive = (
+        ref.at[0] for ref in (disp, spec, cen, nbr, cnt, alive)
+    )
+    total = result.at[pl.ds(0, CELLS * CELLS)]
     me = tuple(lax.axis_index(a) for a in AXES)
 
     def peer(step, sign):
@@ -255,8 +265,8 @@
         return out, kind
 
     def fetch(block, onehot):
-        hi, lo = halves(block.T)
-        return raw(hi, onehot, NN) + raw(lo, onehot, NN)
+        both = raw(jnp.concatenate(halves(block.T), axis=0), onehot, NN)
+        return both[:LANES] + both[LANES:]
 
     place_i, place_j = z_i * 3.0 + atom_i, z_in * 3.0 + atom_j
     shift_i, kind_i = picked(fetch(table[pl.ds(0, own), :], hot_i), place_i)
@@ -344,7 +354,8 @@
     column = jnp.broadcast_to(readout[...], (8, width)).T[:, 0:1]
     score = jnp.sum(column * updated, axis=0, keepdims=True)
     pair_energy = score * scale
-    energy[...] = mm_exact_b(jnp.broadcast_to(pair_energy, (8, pairs)), mine16, NT)[0:1]
+    energies = mm_exact_b(jnp.broadcast_to(pair_energy, (8, pairs)), mine16, NT)
+    result[pl.ds(CELLS * CELLS, 8), 0:centre_total] = energies
 
     d_out = (column * scale) * updated_d
     back = mm(out_t.T, d_out)
@@ -386,7 +397,7 @@
             [out, jnp.zeros((LANES - ZROWS, pairs), jnp.float32)], axis=0
         )
 
-    part[...] = mm_exact_a(hot_j, placed(place_j, -1.0), NT)
+    part[...] = mm_exact_a(hot_j, placed(place_j, -1.0))
     for dx, dy, dz, tile, tiles in plan:
         copy = pltpu.make_async_remote_copy(
             src_ref=part.at[pl.ds(8 * tile, 8 * tiles)],
@@ -397,7 +408,7 @@
             device_id_type=pl.DeviceIdType.MESH,
         )
         copy.start()
-    total[...] = part[pl.ds(0, own), :] + mm_exact_a(hot_i, placed(place_i, 1.0), NT)
+    total[...] = part[pl.ds(0, own), :] + mm_exact_a(hot_i, placed(place_i, 1.0))
     settle(got, send_b, recv_b)
     for dx, dy, dz, tile, tiles in plan:
         if dx == 0 and dy != 0:
@@ -407,11 +418,16 @@
         else:
             spot = pl.ds(8 * origin(dx, tiles), 8 * tiles)
             total[spot, :] = total[spot, :] + got[pl.ds(8 * tile, 8 * tiles), :]
+
+
+def unpack_body(result, energy, forces):
+    energy[0] = result[pl.ds(CELLS * CELLS, 1), 0 : energy.shape[2]]
     final = jnp.concatenate(
-        [total[pl.ds(j, 4, stride=16), :][:, 0:ZROWS] for j in range(16)], axis=1
-    )
+        [result[pl.ds(j, 4, stride=16), :][:, 0:ZROWS] for j in range(16)], axis=1
+    )
+    wide = 16 * ZROWS
     for q in range(4):
-        forces[:, dwide * q : dwide * (q + 1)] = final[q : q + 1, :]
+        forces[0, :, wide * q : wide * (q + 1)] = final[q : q + 1, :]
 
 
 def solution(mesh):
@@ -432,26 +448,31 @@
         def body(*refs):
             kernel_body(sizes, plan, *refs)
 
-        return pl.pallas_call(
+        result = pl.pallas_call(
             body,
-            out_shape=(
-                jax.ShapeDtypeStruct(centres.shape, jnp.float32),
-                jax.ShapeDtypeStruct(displacement.shape, jnp.float32),
-            ),
+            out_shape=jax.ShapeDtypeStruct((CELLS * CELLS + 8, LANES), jnp.float32),
             in_specs=[pl.BlockSpec(memory_space=pltpu.HBM)] * len(args),
-            out_specs=(vmem, vmem),
+            out_specs=vmem,
             scratch_shapes=[pltpu.VMEM(x.shape, x.dtype) for x in args]
             + [
                 pltpu.VMEM((rows, LANES), jnp.float32),
                 pltpu.VMEM((32, LANES), jnp.float32),
                 pltpu.VMEM((rows, LANES), jnp.float32),
                 pltpu.VMEM((rows, LANES), jnp.float32),
-                pltpu.VMEM((CELLS * CELLS, LANES), jnp.float32),
             ]
             + [pltpu.SemaphoreType.DMA((1,))] * 4
             + [pltpu.SemaphoreType.DMA((len(args),))],
             compiler_params=pltpu.CompilerParams(collective_id=0, has_side_effects=True),
         )(*args)
+        return pl.pallas_call(
+            unpack_body,
+            out_shape=(
+                jax.ShapeDtypeStruct(centres.shape, jnp.float32),
+                jax.ShapeDtypeStruct(displacement.shape, jnp.float32),
+            ),
+            in_specs=[vmem],
+            out_specs=(vmem, vmem),
+        )(result)
 
     split = P(*AXES)
     return jax.shard_map(

time: 26.1 us -> 24.3 us (0.931)
  local copies, waits for them, and re-layouts: 2.47 us -> 0 us
  Pallas kernels: 22.1 us -> 22.8 us
    unnamed x4 -> x0, local copies, waits for them, and re-layouts: 2.47 us -> none
    pallas_call x1 -> x2, Pallas kernels: 22.1 us -> 22.8 us  [the longest x1 21.4 us: local(): pl.pallas_call(body, out_shape=jax.ShapeDtypeStruct((CELLS * CELLS + 8, L...]
where the time goes in v3:
time: 24.3 us; the launch traced here: 24.1 us
  Pallas kernels  22.8 us (94%)
  between operations  1.29 us (5%)
    pallas_call x1, Pallas kernels, local(): pl.pallas_call(body, out_shape=jax.ShapeDtypeStruct((CELLS * CELLS + 8, L...  21.4 us
    pallas_call x1, Pallas kernels, local(): pl.pallas_call(unpack_body, out_shape=(jax.ShapeDtypeStruct(centres.shape...  1.47 us

profile of v3, /device:TPU:0, one launch (start us, length us, event | category | flops | bytes accessed | tf_op | source)
XLA Modules:
  0.0 24.1 jit_solution(10127456745397200437)
XLA Ops:
  1.3 21.4 %shard_map.122.result = f32[72,128]{1,0:T(8,128)} custom-call(f32[1,1,4608]{2,1,0:T(1,128)} %refs_0_.1, s32[1,1,1536]{2,1,0:T(1,128)} %refs_1_.1, s32[1,1,16]{2,1,0:T(1,128)} %refs_2_.1, s32[1,1,512]{2,1,0:T(1,128)} %refs_3_.1, s32[1,1,16]{2,1,0:T(1,128)} %refs_4_.1, s32[1,1,1]{2,1,0:T(1,128)S(6)} %copy.13.refs_5_, f32[12,64]{1,0:T(8,128)} %refs_6_.1, ...), custom_call_target="tpu_custom_call" | custom-call | tf_op jit(solution)/shard_map/pallas_call | solution.py:451
  22.6 1.5 %shard_map.123 = (f32[1,1,16]{2,1,0:T(1,128)}, f32[1,1,4608]{2,1,0:T(1,128)}) custom-call(f32[72,128]{1,0:T(8,128)} %shard_map.122.result), custom_call_target="tpu_custom_call" | custom-call | tf_op jit(solution)/shard_map/pallas_call | solution.py:467
